TPU v7x, 32 devices: a whole 2x2x4 slice. The times are simulated.
32 devices in a mesh: dp: 4 (over x, core), mp: 8 (over z, y).
Axes of the slice: x: 2, y: 2, z: 4, core: 2. Of those that a mesh axis runs over, the one named last changes fastest.
Arguments:
- tokens: bfloat16 [1280, 1792], P(('dp', 'mp')), may hold values from -6 to 6
- norm_gain: float32 [1792], replicated, may hold values from 0.5 to 1.5
- norm_bias: float32 [1792], replicated, may hold values from -3 to 3
- w_in: bfloat16 [1792, 15360], P('dp', 'mp'), may hold values from -0.125 to 0.125
- b_in: float32 [15360], P('mp'), may hold values from -3 to 3
- w_out: bfloat16 [15360, 1792], P('mp', 'dp'), may hold values from -0.046875 to 0.046875
- b_out: float32 [1792], replicated, may hold values from -3 to 3
Outputs:
- result: bfloat16 [1280, 1792], P(('dp', 'mp'))
All inputs are finite; a program needn't handle non-finite values.
Results may differ from a plain program's by a relative error of at most 0.0042.
Values may be sent and summed in bfloat16 or wider, within the bound.
A program may use at most 128 MiB of HBM per device.

v0:
```python
import jax
import jax.numpy as jnp
from jax import lax
from jax.sharding import PartitionSpec as P


def on_device(tokens, norm_gain, norm_bias, w_in, b_in, w_out, b_out):
    values = tokens.astype(jnp.float32)
    center = jnp.mean(values, axis=1, keepdims=True)
    spread = jnp.mean((values - center) ** 2, axis=1, keepdims=True)
    normed = ((values - center) / jnp.sqrt(spread + 1e-06) * norm_gain + norm_bias).astype(
        jnp.bfloat16
    )
    w_in_full = lax.all_gather(w_in, "dp", axis=0, tiled=True)
    gathered = lax.all_gather(normed, "mp", axis=0, tiled=True)
    pre = jnp.dot(gathered, w_in_full, preferred_element_type=jnp.float32) + b_in
    hidden = jax.nn.gelu(pre, approximate=False).astype(jnp.bfloat16)
    w_out_full = lax.all_gather(w_out, "dp", axis=1, tiled=True)
    summed = lax.psum_scatter(
        jnp.dot(hidden, w_out_full, preferred_element_type=jnp.float32),
        "mp",
        scatter_dimension=0,
        tiled=True,
    )
    return (values + summed + b_out).astype(jnp.bfloat16)


def solution(mesh):
    placed = (P(("dp", "mp"), None), P(), P(), P("dp", "mp"), P("mp"), P("mp", "dp"), P())
    return jax.shard_map(
        on_device, mesh=mesh, in_specs=placed, out_specs=P(("dp", "mp"), None), check_vma=False
    )
```

profile of v0, /device:TPU:0, one launch (start us, length us, event | category | flops | bytes accessed | tf_op | source)
XLA Modules:
  0.0 249.3 jit_solution(16586171305829466705)
XLA Ops:
  6.5 0.0 copy-start.2
  6.5 0.0 all-gather.4.cloned.1.call-start
  6.5 1.0 convert_reduce_fusion
  7.6 1.1 fusion.45
  8.7 1.7 fusion.48
  10.5 0.0 all-gather.4.cloned.1.call-update
  10.5 0.0 all-gather.6.cloned.1.call-start
  10.5 0.7 all-gather.6.cloned.1.call-update
  11.2 0.0 all-gather.8.cloned.1.call-start
  11.3 0.7 all-gather.8.cloned.1.call-update
  12.0 0.0 copy-start
  12.0 0.0 copy-start.1
  12.0 0.0 reduce-scatter.2.cloned.1.call-start
  12.0 42.5 %all-gather.4.cloned.1.call-done = bf16[320,1792]{1,0:T(8,128)(2,1)} async-done(((bf16[40,1792]{1,0:T(8,128)(2,1)}), bf16[320,1792]{1,0:T(8,128)(2,1)}) %all-gather.4.cloned.1.call-update) | async-done | bytes 1146896 | tf_op jit(solution)/shard_map/all_gather | solution.py:15
  54.6 49.7 %all-gather.6.cloned.1.call-done = bf16[1792,1920]{1,0:T(8,128)(2,1)} async-done(((bf16[448,1920]{1,0:T(8,128)(2,1)}), bf16[1792,1920]{1,0:T(8,128)(2,1)}) %all-gather.6.cloned.1.call-update) | async-done | bytes 6881296 | tf_op jit(solution)/shard_map/all_gather | solution.py:14
  104.3 51.3 %all-gather.8.cloned.1.call-done = bf16[1920,1792]{0,1:T(8,128)(2,1)} async-done(((bf16[1920,448]{0,1:T(8,128)(2,1)}), bf16[1920,1792]{0,1:T(8,128)(2,1)}) %all-gather.8.cloned.1.call-update) | async-done | bytes 6881296 | tf_op jit(solution)/shard_map/all_gather | solution.py:18
  155.6 0.0 copy-done.2
  155.6 15.7 %fusion.10 = f32[320,1792]{1,0:T(8,128)} fusion(bf16[1920,1792]{0,1:T(8,128)(2,1)} %all-gather.8.cloned.1.call-done, bf16[320,1792]{1,0:T(8,128)(2,1)} %all-gather.4.cloned.1.call-done, bf16[1792,1920]{1,0:T(8,128)(2,1)} %all-gather.6.cloned.1.call-done, f32[1920]{0:T(1024)S(1)} %copy-done.2), kind=kOutput, calls=%fused_computation.20 | convolution fusion | flops 4444569600 | bytes 17210880 | tf_op jit(solution)/shard_map/dot_general | solution.py:20
  171.3 0.0 reduce-scatter.2.cloned.1.call-update
  171.4 69.7 %reduce-scatter.2.cloned.1.call-done = f32[40,1792]{1,0:T(8,128)} async-done(((f32[320,1792]{1,0:T(8,128)}), f32[40,1792]{1,0:T(8,128)}) %reduce-scatter.2.cloned.1.call-update) | async-done | bytes 286736 | tf_op jit(solution)/shard_map/reduce_scatter | solution.py:19
  241.1 0.0 copy-done
  241.1 0.0 copy-done.1
  241.1 1.7 fusion.50
  (2 shorter events, 0.0 us)
Async XLA Ops:
  6.5 149.1 %copy-start.2 = (f32[1920]{0:T(1024)S(1)}, f32[1920]{0:T(1024)}, u32[]{:S(2)}) copy-start(f32[1920]{0:T(1024)} %param.11) | copy-start | bytes 23044
  6.5 48.0 %all-gather.4.cloned.1.call-start = ((), (), s32[]{:S(2)}) async-start(), calls=%async_computation.1 | async-start | bytes 1290240 | tf_op jit(solution)/shard_map/all_gather | solution.py:15
  10.5 93.8 %all-gather.6.cloned.1.call-start = ((), (), s32[]{:S(2)}) async-start(), calls=%async_computation.2 | async-start | bytes 8601600 | tf_op jit(solution)/shard_map/all_gather | solution.py:14
  11.2 144.4 %all-gather.8.cloned.1.call-start = ((), (), s32[]{:S(2)}) async-start(), calls=%async_computation.3 | async-start | bytes 8601600 | tf_op jit(solution)/shard_map/all_gather | solution.py:18
  12.0 229.1 %copy-start = (bf16[40,1792]{1,0:T(8,128)(2,1)S(1)}, bf16[40,1792]{1,0:T(8,128)(2,1)}, u32[]{:S(2)}) copy-start(bf16[40,1792]{1,0:T(8,128)(2,1)} %param.7) | copy-start | bytes 430084
  12.0 229.1 %copy-start.1 = (f32[1792]{0:T(1024)S(1)}, f32[1792]{0:T(1024)}, u32[]{:S(2)}) copy-start(f32[1792]{0:T(1024)} %param.13) | copy-start | bytes 21508
  12.0 229.1 %reduce-scatter.2.cloned.1.call-start = ((), (), s32[]{:S(2)}) async-start(), calls=%async_computation.4 | async-start | bytes 2580480 | tf_op jit(solution)/shard_map/reduce_scatter | solution.py:19
Sparse Core Ops, SparseCore 0:
  10.6 43.9 all-gather.3
  56.1 48.1 all-gather.5
  105.9 49.6 all-gather.7
  171.5 69.5 reduce-scatter.1
where the time goes:
time: 249 us
  waiting for transfers between devices  215 us (86%)
  matrix products  15.7 us (6%)
  between operations  13.2 us (5%)
  other arithmetic  5.56 us (2%)
    reduce_scatter x1, waiting for transfers between devices, on_device(): lax.psum_scatter(jnp.dot(hidden, w_out_full, preferred_element_type=jnp.f...  69.7 us
    all_gather x1, waiting for transfers between devices, on_device(): w_out_full = lax.all_gather(w_out, 'dp', axis=1, tiled=True)  51.3 us
    all_gather x1, waiting for transfers between devices, on_device(): w_in_full = lax.all_gather(w_in, 'dp', axis=0, tiled=True)  49.7 us
    all_gather x1, waiting for transfers between devices, on_device(): gathered = lax.all_gather(normed, 'mp', axis=0, tiled=True)  42.5 us
    dot_general x1, matrix products, on_device(): jnp.dot(hidden, w_out_full, preferred_element_type=jnp.float32)  15.7 us
  transfers between devices with their start and end apart: 4, of which 4 were waited for; matrix products, arithmetic and copies ran while one was open for 0% of the time, Pallas kernels for 0%

commit v1 on v0

--- a/solution.py
+++ b/solution.py
@@ -2,6 +2,7 @@
 import jax.numpy as jnp
 from jax import lax
 from jax.sharding import PartitionSpec as P
+from jax.lax import all_gather
 
 
 def on_device(tokens, norm_gain, norm_bias, w_in, b_in, w_out, b_out):
@@ -15,7 +16,7 @@
     gathered = lax.all_gather(normed, "mp", axis=0, tiled=True)
     pre = jnp.dot(gathered, w_in_full, preferred_element_type=jnp.float32) + b_in
     hidden = jax.nn.gelu(pre, approximate=False).astype(jnp.bfloat16)
-    w_out_full = lax.all_gather(w_out, "dp", axis=1, tiled=True)
+    w_out_full = jnp.concatenate(all_gather(w_out, "dp"), axis=1)
     summed = lax.psum_scatter(
         jnp.dot(hidden, w_out_full, preferred_element_type=jnp.float32),
         "mp",

time: 249 us -> 249 us (level)
  waiting for transfers between devices: 215 us -> 195 us
  local copies, waits for them, and re-layouts: 0.02 us -> 18.9 us
    all_gather x1, waiting for transfers between devices: 42.5 us -> 24.5 us  [on_device(): gathered = lax.all_gather(normed, 'mp', axis=0, tiled=True)]
    all_gather x0 -> x1, local copies, waits for them, and re-layouts: none -> 12.2 us  [on_device(): w_out_full = jnp.concatenate(all_gather(w_out, 'dp'), axis=1)]
    reshape x0 -> x1, local copies, waits for them, and re-layouts: none -> 6.71 us  [on_device(): w_out_full = jnp.concatenate(all_gather(w_out, 'dp'), axis=1)]
  transfers between devices with their start and end apart: 4 -> 4, of which waited for: 4 -> 4; matrix products, arithmetic and copies ran while one was open for 0% -> 9% of each run, Pallas kernels for 0% -> 0%
where the time goes in v1:
time: 249 us
  waiting for transfers between devices  195 us (78%)
  local copies, waits for them, and re-layouts  18.9 us (8%)
  matrix products  15.8 us (6%)
  between operations  13.1 us (5%)
  other arithmetic  5.55 us (2%)
    reduce_scatter x1, waiting for transfers between devices, on_device(): lax.psum_scatter(jnp.dot(hidden, w_out_full, preferred_element_type=jnp.f...  70 us
    all_gather x1, waiting for transfers between devices, on_device(): w_in_full = lax.all_gather(w_in, 'dp', axis=0, tiled=True)  49.7 us
    all_gather x1, waiting for transfers between devices, on_device(): w_out_full = jnp.concatenate(all_gather(w_out, 'dp'), axis=1)  49.3 us
    all_gather x1, waiting for transfers between devices, on_device(): gathered = lax.all_gather(normed, 'mp', axis=0, tiled=True)  24.5 us
    dot_general x1, matrix products, on_device(): jnp.dot(hidden, w_out_full, preferred_element_type=jnp.float32)  15.8 us
    all_gather x1, local copies, waits for them, and re-layouts, on_device(): w_out_full = jnp.concatenate(all_gather(w_out, 'dp'), axis=1)  12.2 us
    reshape x1, local copies, waits for them, and re-layouts, on_device(): w_out_full = jnp.concatenate(all_gather(w_out, 'dp'), axis=1)  6.71 us
  transfers between devices with their start and end apart: 4, of which 4 were waited for; matrix products, arithmetic and copies ran while one was open for 9% of the time, Pallas kernels for 0%

profile of v1, /device:TPU:0, one launch (start us, length us, event | category | flops | bytes accessed | tf_op | source)
XLA Modules:
  0.0 248.5 jit_solution(16990426359975341822)
XLA Ops:
  6.5 0.0 all-gather.9.cloned.1.call-start
  6.5 0.7 all-gather.9.cloned.1.call-update
  7.3 0.0 all-gather.5.cloned.1.call-start
  7.3 1.0 convert_reduce_fusion
  8.3 1.1 fusion.45
  9.5 1.7 fusion.48
  11.2 0.0 all-gather.5.cloned.1.call-update
  11.2 0.0 all-gather.7.cloned.1.call-start
  11.3 0.7 all-gather.7.cloned.1.call-update
  12.0 0.0 reduce-scatter.2.cloned.1.call-start
  12.0 49.3 %all-gather.9.cloned.1.call-done = bf16[7680,448]{0,1:T(8,128)(2,1)} async-done(((bf16[1920,448]{0,1:T(8,128)(2,1)}), bf16[7680,448]{0,1:T(8,128)(2,1)}) %all-gather.9.cloned.1.call-update) | async-done | bytes 6881296 | tf_op jit(solution)/shard_map/all_gather | solution.py:19
  61.3 12.2 %reshape.24 = bf16[4,1920,448]{1,0,2:T(4,128)(2,1)} reshape(bf16[7680,448]{0,1:T(8,128)(2,1)} %all-gather.9.cloned.1.call-done) | data formatting | bytes 13762560 | tf_op jit(solution)/shard_map/all_gather | solution.py:19
  73.5 0.0 copy-start.2
  73.5 6.7 %copy.8 = bf16[1920,4,448]{0,2,1:T(8,128)(2,1)} copy(bf16[1920,4,448]{0,1,2:T(4,128)(2,1)} %bitcast.7) | data formatting | bytes 13762560 | tf_op jit(solution)/shard_map/reshape | solution.py:19
  80.2 24.5 %all-gather.5.cloned.1.call-done = bf16[320,1792]{1,0:T(8,128)(2,1)} async-done(((bf16[40,1792]{1,0:T(8,128)(2,1)}), bf16[320,1792]{1,0:T(8,128)(2,1)}) %all-gather.5.cloned.1.call-update) | async-done | bytes 1146896 | tf_op jit(solution)/shard_map/all_gather | solution.py:16
  104.7 49.7 %all-gather.7.cloned.1.call-done = bf16[1792,1920]{1,0:T(8,128)(2,1)} async-done(((bf16[448,1920]{1,0:T(8,128)(2,1)}), bf16[1792,1920]{1,0:T(8,128)(2,1)}) %all-gather.7.cloned.1.call-update) | async-done | bytes 6881296 | tf_op jit(solution)/shard_map/all_gather | solution.py:15
  154.5 0.0 copy-done.2
  154.5 0.0 copy-start
  154.5 15.8 %fusion.10 = f32[320,1792]{1,0:T(8,128)} fusion(bf16[1920,1792]{0,1:T(8,128)(2,1)} %bitcast.8, bf16[320,1792]{1,0:T(8,128)(2,1)} %all-gather.5.cloned.1.call-done, bf16[1792,1920]{1,0:T(8,128)(2,1)} %all-gather.7.cloned.1.call-done, f32[1920]{0:T(1024)S(1)} %copy-done.2), kind=kOutput, calls=%fused_computation.20 | convolution fusion | flops 4444569600 | bytes 17210880 | tf_op jit(solution)/shard_map/dot_general | solution.py:21
  170.3 0.0 reduce-scatter.2.cloned.1.call-update
  170.3 70.0 %reduce-scatter.2.cloned.1.call-done = f32[40,1792]{1,0:T(8,128)} async-done(((f32[320,1792]{1,0:T(8,128)}), f32[40,1792]{1,0:T(8,128)}) %reduce-scatter.2.cloned.1.call-update) | async-done | bytes 286736 | tf_op jit(solution)/shard_map/reduce_scatter | solution.py:20
  240.3 0.0 copy-done
  240.3 0.0 copy-done.1
  240.3 1.7 fusion.50
  (3 shorter events, 0.0 us)
Async XLA Ops:
  6.5 54.8 %all-gather.9.cloned.1.call-start = ((), (), s32[]{:S(2)}) async-start(), calls=%async_computation.4 | async-start | bytes 8601600 | tf_op jit(solution)/shard_map/all_gather | solution.py:19
  7.3 97.5 %all-gather.5.cloned.1.call-start = ((), (), s32[]{:S(2)}) async-start(), calls=%async_computation.1 | async-start | bytes 1290240 | tf_op jit(solution)/shard_map/all_gather | solution.py:16
  11.2 143.3 %all-gather.7.cloned.1.call-start = ((), (), s32[]{:S(2)}) async-start(), calls=%async_computation.2 | async-start | bytes 8601600 | tf_op jit(solution)/shard_map/all_gather | solution.py:15
  12.0 228.4 %reduce-scatter.2.cloned.1.call-start = ((), (), s32[]{:S(2)}) async-start(), calls=%async_computation.3 | async-start | bytes 2580480 | tf_op jit(solution)/shard_map/reduce_scatter | solution.py:20
  73.5 81.0 %copy-start.2 = (f32[1920]{0:T(1024)S(1)}, f32[1920]{0:T(1024)}, u32[]{:S(2)}) copy-start(f32[1920]{0:T(1024)} %param.11) | copy-start | bytes 23044
  154.5 85.8 %copy-start = (bf16[40,1792]{1,0:T(8,128)(2,1)S(1)}, bf16[40,1792]{1,0:T(8,128)(2,1)}, u32[]{:S(2)}) copy-start(bf16[40,1792]{1,0:T(8,128)(2,1)} %param.7) | copy-start | bytes 430084
  154.5 85.8 %copy-start.1 = (f32[1792]{0:T(1024)S(1)}, f32[1792]{0:T(1024)}, u32[]{:S(2)}) copy-start(f32[1792]{0:T(1024)} %param.13) | copy-start | bytes 21508
Sparse Core Ops, SparseCore 0:
  8.9 52.3 all-gather.8
  63.5 41.1 all-gather.4
  106.3 48.1 all-gather.6
  170.4 69.8 reduce-scatter.1
